TPU v7x, 32 devices: a whole 2x2x4 slice. The times are simulated.
32 devices in a mesh: gx: 2 (over x), gy: 4 (over z), ta: 4 (over y, core).
Axes of the slice: x: 2, y: 2, z: 4, core: 2. Of those that a mesh axis runs over, the one named last changes fastest.
Arguments:
- traces: bfloat16 [131072, 1024], P(('gx', 'gy'), 'ta'), may hold values from -6 to 6
- interp: bfloat16 [2, 16], replicated, may hold values from -1.5 to 1.5
- translations: bfloat16 [4, 2048, 1024], P(None, ('gx', 'gy')), may hold values from -0.125 to 0.125
- leaf_slot: int32 [8192], P(('gx', 'gy', 'ta')), may hold values from 0 to 255, as said below
- pairing: int32 [4, 8192], P(None, ('gx', 'gy', 'ta')), may hold values from 0 to 255, as said below
Outputs:
- coefficients: bfloat16 [8192, 1024], P(('gx', 'gy', 'ta'))
Inputs may be any that keep to these rules, and one draw needn't show every extreme that they name: `leaf_slot`: each aligned block of 256 entries (the leaves of one device) is a permutation of 0 to 255. `pairing`: for every level, each aligned block of 256 entries along the leaves is a permutation of 0 to 255.
All inputs are finite; a program needn't handle non-finite values.
Results may differ from a plain program's by a relative error of at most 0.0082.
Values may be sent and summed in bfloat16 or wider, within the bound.
A program may use at most 128 MiB of HBM per device.

v0:
```python
import functools
import math

import jax
import jax.numpy as jnp
import numpy as np
from jax import lax
from jax.experimental import pallas as pl
from jax.experimental.pallas import tpu as pltpu
from jax.sharding import PartitionSpec as P

NF = 256
CHEB = 2
BOXT = 16
BLOCK_BOXES = 16
TILE = 256
MESH = pl.DeviceIdType.MESH


def spectrum_table(length, count):
    sample_pos = np.arange(length, dtype=np.float32)[:, None]
    frequency = np.arange(count, dtype=np.float32)[None, :] + np.float32(1.0)
    angles = np.float32(2.0 * math.pi / length) * np.mod(sample_pos * frequency, np.float32(length))
    factor = np.float32(math.sqrt(2.0 / length))
    table = np.concatenate([np.cos(angles) * factor, -np.sin(angles) * factor], axis=1)
    return table.astype(jnp.bfloat16)


def flip(index, mask, size):
    result = index
    bit = 1
    while bit < size:
        if mask & bit:
            result = result + bit - 2 * bit * ((index // bit) % 2)
        bit *= 2
    return result


def kernel(
    sizes,
    traces,
    interp,
    translations,
    slots,
    pairs,
    table,
    out,
    tr,
    weights,
    mat,
    sampled,
    slices,
    fourier,
    acc,
    points,
    arrived,
    states,
    partner,
    select,
    load_sem,
    table_sem,
    own_sem,
    ag_send,
    ag_recv,
    core_send,
    core_recv,
    ta_send,
    ta_recv,
    g_send,
    g_recv,
    level_send,
    level_recv,
):
    n_gx, n_gy, n_ta = sizes
    groups = n_gx * n_gy
    gx, gy, ta = lax.axis_index("gx"), lax.axis_index("gy"), lax.axis_index("ta")
    group = gx * n_gy + gy
    level_count = translations.shape[0]
    rows = translations.shape[1]
    half = rows // 2
    width = translations.shape[2]
    boxes = slots.shape[1]
    span = traces.shape[1]
    block = boxes * BOXT
    chunk = states.shape[3]
    chunks = width // chunk
    log_devices = (groups * n_ta).bit_length() - 1
    side = ta % 2

    def of_group(offset):
        p = flip(group, offset, groups)
        return (p // n_gy, p % n_gy, ta)

    def of_ta(offset):
        return (gx, gy, flip(ta, offset, n_ta))

    def loading(j):
        t = flip(ta, j, n_ta)
        return pltpu.make_async_copy(
            traces.at[pl.ds(pl.multiple_of(t * block, block), block), :], tr.at[j], load_sem.at[j]
        )

    def own(level):
        return [
            pltpu.make_async_copy(
                translations.at[level, pl.ds(part * half, half), :],
                weights.at[level, group, part],
                own_sem.at[level, part],
            )
            for part in range(2)
        ]

    bits = []
    bit = n_gy // 2
    while bit:
        bits.append(bit)
        bit //= 2
    bit = n_gx // 2
    while bit:
        bits.append(bit * n_gy)
        bit //= 2
    stage_of = {0: -1}
    order = [0]
    for stage, bit in enumerate(bits):
        for offset in list(order):
            stage_of[offset ^ bit] = stage
            order.append(offset ^ bit)

    def shard(level, offset):
        return weights.at[level, flip(group, offset, groups), side]

    def passing(level, offset, stage):
        bit = bits[stage]
        return pltpu.make_async_remote_copy(
            src_ref=shard(level, offset),
            dst_ref=shard(level, offset),
            send_sem=ag_send.at[level, offset ^ bit],
            recv_sem=ag_recv.at[level, offset ^ bit],
            device_id=of_group(bit),
            device_id_type=MESH,
        )

    def landed(level, offset):
        bit = bits[stage_of[offset]]
        return pltpu.make_async_remote_copy(
            src_ref=shard(level, offset),
            dst_ref=shard(level, offset),
            send_sem=ag_send.at[level, offset],
            recv_sem=ag_recv.at[level, offset],
            device_id=of_group(bit),
            device_id_type=MESH,
        )

    def sharing(level, offset, mine):
        place = weights.at[
            level, flip(group, offset, groups), side if mine else flip(side, 1, 2)
        ]
        return pltpu.make_async_remote_copy(
            src_ref=place,
            dst_ref=place,
            send_sem=core_send.at[level, offset],
            recv_sem=core_recv.at[level, offset],
            device_id=of_ta(1),
            device_id_type=MESH,
        )

    def pump(level, stage):
        if stage == 0:
            for copy in own(level):
                copy.wait()
        for offset in order:
            if stage_of[offset] != stage - 1:
                continue
            if offset:
                landed(level, offset).wait_recv()
                sharing(level, offset, True).start()
            for later in range(stage, len(bits)):
                passing(level, offset, later).start()

    stages = len(bits)

    reached = [0]

    def pumps(step):
        while reached[0] <= step:
            for level in range(level_count):
                stage = reached[0] - level
                if 0 <= stage <= stages:
                    pump(level, stage)
            reached[0] += 1

    def finish(level):
        for offset in order[1:]:
            sharing(level, offset, False).wait_recv()

    def regroup(j):
        return pltpu.make_async_remote_copy(
            src_ref=sampled.at[j],
            dst_ref=slices.at[j],
            send_sem=ta_send.at[j],
            recv_sem=ta_recv.at[j],
            device_id=of_ta(j),
            device_id_type=MESH,
        )

    def moving(offset, sending):
        src = points.at[flip(group, offset, groups)]
        dst = arrived.at[group if sending else flip(group, offset, groups)]
        return pltpu.make_async_remote_copy(
            src_ref=src,
            dst_ref=dst,
            send_sem=g_send.at[offset],
            recv_sem=g_recv.at[offset],
            device_id=of_group(offset),
            device_id_type=MESH,
        )

    def exchange(level, k):
        mask = 2 ** (level * log_devices // level_count)
        target = of_ta(mask) if mask < n_ta else of_group(mask // n_ta)
        return pltpu.make_async_remote_copy(
            src_ref=states.at[level, k],
            dst_ref=partner.at[level, k],
            send_sem=level_send.at[level, k],
            recv_sem=level_recv.at[level, k],
            device_id=target,
            device_id_type=MESH,
        )

    near = [n_ta - 1 - j for j in range(n_ta)]
    for j in near:
        loading(j).start()
    for level in range(level_count):
        for copy in own(level):
            copy.start()
    table_copy = pltpu.make_async_copy(table, fourier, table_sem)
    table_copy.start()

    barrier = pltpu.get_barrier_semaphore()
    for j in range(1, n_ta):
        pl.semaphore_signal(barrier, inc=1, device_id=of_ta(j), device_id_type=MESH)
    for offset in range(1, groups):
        pl.semaphore_signal(barrier, inc=1, device_id=of_group(offset), device_id_type=MESH)

    columns = BLOCK_BOXES * BOXT
    spread = (
        lax.broadcasted_iota(jnp.int32, (BOXT, columns), 1) % BOXT
        == lax.broadcasted_iota(jnp.int32, (BOXT, columns), 0)
    )
    tiled = jnp.dot(
        interp[...], spread.astype(jnp.float32).astype(jnp.bfloat16), preferred_element_type=jnp.float32
    )
    own_box = (
        lax.broadcasted_iota(jnp.int32, (BLOCK_BOXES, columns), 1) // BOXT
        == lax.broadcasted_iota(jnp.int32, (BLOCK_BOXES, columns), 0)
    )
    for c in range(CHEB):
        mat[pl.ds(c * BLOCK_BOXES, BLOCK_BOXES), :] = jnp.where(
            own_box, tiled[c : c + 1, :], 0.0
        ).astype(jnp.bfloat16)

    def selection(index_row):
        hit = lax.broadcasted_iota(jnp.int32, (boxes, boxes), 0) == index_row
        return jnp.where(hit, 1.0, 0.0).T.astype(jnp.bfloat16)

    select[0] = selection(slots[...])
    for level in range(level_count):
        select[level + 1] = selection(pairs[pl.ds(level, 1), :])

    pl.semaphore_wait(barrier, n_ta - 1 + groups - 1)
    pumps(0)

    for j in near:
        loading(j).wait()
        where = sampled if j else slices

        def interpolate(i, carry):
            traces_block = tr[j, pl.ds(pl.multiple_of(i * columns, columns), columns), :]
            both = jnp.dot(mat[...], traces_block, preferred_element_type=jnp.float32)
            both = both.astype(jnp.bfloat16)
            place = pl.ds(pl.multiple_of(i * BLOCK_BOXES, BLOCK_BOXES), BLOCK_BOXES)
            for c in range(CHEB):
                where[j, c, place, :] = both[c * BLOCK_BOXES : (c + 1) * BLOCK_BOXES, :]
            return carry

        lax.fori_loop(0, boxes // BLOCK_BOXES, interpolate, 0, unroll=4)
        if j:
            regroup(j).start()

    pumps(1)
    table_copy.wait()
    for j in range(n_ta):
        if j:
            regroup(j).wait_recv()
        first = pl.multiple_of(flip(ta, j, n_ta) * span, span)
        for c in range(CHEB):
            part = jnp.dot(
                slices[j, c], fourier[pl.ds(first, span), :], preferred_element_type=jnp.float32
            )
            cols = pl.ds(c * 2 * NF, 2 * NF)
            if j:
                acc[:, cols] += part
            else:
                acc[:, cols] = part
    points[...] = acc[...].reshape(points.shape).astype(jnp.bfloat16)
    for offset in range(groups - 1, 0, -1):
        moving(offset, True).start()
    arrived[group] = points[group]
    pumps(2)
    for offset in range(1, groups):
        moving(offset, False).wait_recv()

    for k in range(chunks):
        boxes_in = arrived[:, :, k * chunk : (k + 1) * chunk].astype(jnp.float32)
        boxes_in = boxes_in.reshape(boxes, chunk).astype(jnp.bfloat16)
        states[0, k] = jnp.dot(select[0], boxes_in, preferred_element_type=jnp.float32).astype(
            jnp.bfloat16
        )
        exchange(0, k).start()

    per_chunk = chunk // rows

    def weight(level, k, cols):
        piece = weights[level, k * per_chunk : (k + 1) * per_chunk, :, :, cols]
        return piece.reshape(chunk, chunk)

    for level in range(level_count):
        pumps(level + stages)
        finish(level)

        def own_part(n, carry):
            cols = pl.ds(pl.multiple_of(n * chunk, chunk), chunk)
            total = jnp.zeros((boxes, chunk), jnp.float32)
            for k in range(chunks):
                total += jnp.dot(
                    states[level, k], weight(level, k, cols), preferred_element_type=jnp.float32
                )
            acc[:, cols] = total
            return carry

        lax.fori_loop(0, chunks, own_part, 0)
        for k in range(chunks):
            exchange(level, k).wait_recv()
            aligned = jnp.dot(
                select[level + 1], partner[level, k], preferred_element_type=jnp.float32
            ).astype(jnp.bfloat16)
            if k < chunks - 1:

                def partner_part(n, carry):
                    cols = pl.ds(pl.multiple_of(n * chunk, chunk), chunk)
                    acc[:, cols] += jnp.dot(
                        aligned, weight(level, chunks + k, cols), preferred_element_type=jnp.float32
                    )
                    return carry

                lax.fori_loop(0, chunks, partner_part, 0)
            else:
                for n in range(chunks):
                    cols = pl.ds(n * chunk, chunk)
                    total = acc[:, cols] + jnp.dot(
                        aligned, weight(level, chunks + k, cols), preferred_element_type=jnp.float32
                    )
                    if level < level_count - 1:
                        states[level + 1, n] = total.astype(jnp.bfloat16)
                        exchange(level + 1, n).start()
                    else:
                        out[:, cols] = total.astype(jnp.bfloat16)

    for j in range(1, n_ta):
        regroup(j).wait_send()
    for offset in range(1, groups):
        moving(offset, True).wait_send()
    for level in range(level_count):
        for k in range(chunks):
            exchange(level, k).wait_send()
        for offset in order[1:]:
            landed(level, offset).wait_send()
            sharing(level, offset, True).wait_send()


def on_device(sizes, traces, interp, translations, leaf_slot, pairing):
    n_gx, n_gy, n_ta = sizes
    groups = n_gx * n_gy
    boxes = leaf_slot.shape[0]
    levels, rows, width = translations.shape
    span = traces.shape[1]
    block = traces.shape[0] // n_ta
    chunk = max(TILE, rows)
    chunks = width // chunk
    table = jnp.asarray(spectrum_table(span * n_ta, NF))
    bf16, f32 = jnp.bfloat16, jnp.float32
    anywhere = pl.BlockSpec(memory_space=pl.ANY)
    vmem = pl.BlockSpec(memory_space=pltpu.VMEM)
    dma = pltpu.SemaphoreType.DMA
    return pl.pallas_call(
        functools.partial(kernel, sizes),
        out_shape=jax.ShapeDtypeStruct((boxes, width), bf16),
        in_specs=[anywhere, vmem, anywhere, vmem, vmem, anywhere],
        out_specs=vmem,
        scratch_shapes=[
            pltpu.VMEM((n_ta, block, span), bf16),
            pltpu.VMEM((levels, groups, 2, rows // 2, width), bf16),
            pltpu.VMEM((CHEB * BLOCK_BOXES, BLOCK_BOXES * BOXT), bf16),
            pltpu.VMEM((n_ta, CHEB, boxes, span), bf16),
            pltpu.VMEM((n_ta, CHEB, boxes, span), bf16),
            pltpu.VMEM(table.shape, bf16),
            pltpu.VMEM((boxes, width), f32),
            pltpu.VMEM((groups, boxes // groups, width), bf16),
            pltpu.VMEM((groups, boxes // groups, width), bf16),
            pltpu.VMEM((levels, chunks, boxes, chunk), bf16),
            pltpu.VMEM((levels, chunks, boxes, chunk), bf16),
            pltpu.VMEM((levels + 1, boxes, boxes), bf16),
            dma((n_ta,)),
            dma,
            dma((levels, 2)),
            dma((levels, groups)),
            dma((levels, groups)),
            dma((levels, groups)),
            dma((levels, groups)),
            dma((n_ta,)),
            dma((n_ta,)),
            dma((groups,)),
            dma((groups,)),
            dma((levels, chunks)),
            dma((levels, chunks)),
        ],
        compiler_params=pltpu.CompilerParams(
            collective_id=0, has_side_effects=True, vmem_limit_bytes=60 * 2**20
        ),
    )(traces, interp, translations, leaf_slot.reshape(1, boxes), pairing, table)


def solution(mesh):
    sizes = (mesh.shape["gx"], mesh.shape["gy"], mesh.shape["ta"])
    in_specs = (
        P(("gx", "gy"), "ta"),
        P(),
        P(None, ("gx", "gy"), None),
        P(("gx", "gy", "ta")),
        P(None, ("gx", "gy", "ta")),
    )
    out_specs = P(("gx", "gy", "ta"), None)
    return jax.shard_map(
        functools.partial(on_device, sizes),
        mesh=mesh,
        in_specs=in_specs,
        out_specs=out_specs,
        check_vma=False,
    )
```

profile of v0, /device:TPU:0, one launch (start us, length us, event | category | flops | bytes accessed | tf_op | source)
XLA Modules:
  0.0 126.4 jit_solution(156943696915368910)
XLA Ops:
  0.0 124.5 %shard_map.64 = bf16[256,1024]{1,0:T(8,128)(2,1)} custom-call(bf16[16384,256]{1,0:T(8,128)(2,1)} %traces.1, bf16[2,16]{1,0:T(2,128)(2,1)} %interp.1, bf16[4,256,1024]{2,1,0:T(8,128)(2,1)} %translations.1, s32[1,256]{1,0:T(1,128)} %bitcast.1, s32[4,256]{1,0:T(4,128)} %pairs.1, bf16[1024,512]{1,0:T(8,128)(2,1)} %constant.2.clone.table), custom_call_target="tpu_custom_call" | custom-call | tf_op jit(solution)/shard_map/pallas_call | solution.py:395
  124.5 1.9 %copy.8 = bf16[256,1024]{1,0:T(8,128)(2,1)} copy(bf16[256,1024]{1,0:T(8,128)(2,1)} %shard_map.64) | data formatting | bytes 1048576
where the time goes:
time: 127 us; the launch traced here: 126 us
  Pallas kernels  124 us (98%)
  local copies, waits for them, and re-layouts  1.87 us (1%)
    pallas_call x1, Pallas kernels, on_device(): pl.pallas_call(functools.partial(kernel, sizes), out_shape=jax.ShapeDtype...  124 us

commit v1 on v0

--- a/solution.py
+++ b/solution.py
@@ -15,6 +15,18 @@
 BLOCK_BOXES = 16
 TILE = 256
 MESH = pl.DeviceIdType.MESH
+KEPT = (0.625, 0.625, 0.75, 0.75)
+SCHEDULE = {
+    "start": ((0, 0), (1, 0)),
+    "interp0": ((0, 1),),
+    "table2": ((1, 1),),
+    "spread": ((0, 2), (2, 0), (1, 1), (0, 3), (1, 2), (0, 4), (2, 1)),
+    "level0.0": ((1, 3), (3, 0)),
+    "level1.0": ((2, 2), (3, 1)),
+    "level1.1": ((2, 3),),
+    "level1.2": ((3, 2),),
+    "level2.0": ((3, 3),),
+}
 
 
 def spectrum_table(length, count):
@@ -62,6 +74,10 @@
     own_sem,
     ag_send,
     ag_recv,
+    z_send,
+    x_send,
+    y_send,
+    y_recv,
     core_send,
     core_recv,
     ta_send,
@@ -110,88 +126,184 @@
             for part in range(2)
         ]
 
-    bits = []
-    bit = n_gy // 2
-    while bit:
-        bits.append(bit)
-        bit //= 2
+    xbits = []
     bit = n_gx // 2
     while bit:
-        bits.append(bit * n_gy)
+        xbits.append(bit)
         bit //= 2
     stage_of = {0: -1}
-    order = [0]
-    for stage, bit in enumerate(bits):
-        for offset in list(order):
+    for stage, bit in enumerate(xbits):
+        for offset in list(stage_of):
             stage_of[offset ^ bit] = stage
-            order.append(offset ^ bit)
-
-    def shard(level, offset):
-        return weights.at[level, flip(group, offset, groups), side]
-
-    def passing(level, offset, stage):
-        bit = bits[stage]
-        return pltpu.make_async_remote_copy(
-            src_ref=shard(level, offset),
-            dst_ref=shard(level, offset),
-            send_sem=ag_send.at[level, offset ^ bit],
-            recv_sem=ag_recv.at[level, offset ^ bit],
-            device_id=of_group(bit),
-            device_id_type=MESH,
-        )
-
-    def landed(level, offset):
-        bit = bits[stage_of[offset]]
-        return pltpu.make_async_remote_copy(
-            src_ref=shard(level, offset),
-            dst_ref=shard(level, offset),
-            send_sem=ag_send.at[level, offset],
-            recv_sem=ag_recv.at[level, offset],
-            device_id=of_group(bit),
-            device_id_type=MESH,
-        )
-
-    def sharing(level, offset, mine):
-        place = weights.at[
-            level, flip(group, offset, groups), side if mine else flip(side, 1, 2)
-        ]
+    lines = {offset: flip(gx, offset, n_gx) for offset in stage_of}
+    shards = [
+        (offset, d, k)
+        for k in range(-1, n_gy - 1)
+        for d in ((1,) if k < 0 else (1, -1))
+        for offset in stage_of
+    ]
+    twins = n_ta >= 4
+    twin = flip(ta, 2, n_ta) if twins else ta
+    upper = (ta // 2) % 2
+
+    def kept(level):
+        if not twins:
+            return half
+        return max(half // 2, round(half * KEPT[level % len(KEPT)] / 16) * 16)
+
+    def shard_id(offset, d, k):
+        return lines[offset] * n_gy + gy - d * (k + 1)
+
+    within = {
+        (d, k): gy >= k + 1 if d > 0 else gy < n_gy - 1 - k
+        for d in (1, -1)
+        for k in range(n_gy - 1)
+    }
+    ahead = {1: gy < n_gy - 1, -1: gy > 0}
+
+    def inside(d, k):
+        return None if k < 0 else within[d, k]
+
+    def both(a, b):
+        if a is None or b is None:
+            return b if a is None else a
+        return jnp.logical_and(a, b)
+
+    def guarded(condition, action):
+        if condition is None:
+            action()
+        else:
+            pl.when(condition)(action)
+
+    started = []
+
+    def launch(condition, make, outer=None):
+        guarded(condition, lambda: make().start())
+        started.append((outer, condition, make))
+
+    def in_rows(level):
+        size = kept(level)
+        if size == half:
+            return pl.ds(0, half)
+        return pl.ds(pl.multiple_of(upper * (half - size), 16), size)
+
+    def in_plane(level, shard, sem_ref, sem_at, target):
+        place = weights.at[level, shard, side, in_rows(level), :]
         return pltpu.make_async_remote_copy(
             src_ref=place,
             dst_ref=place,
-            send_sem=core_send.at[level, offset],
-            recv_sem=core_recv.at[level, offset],
+            send_sem=sem_ref.at[sem_at],
+            recv_sem=ag_recv.at[level, shard],
+            device_id=target,
+            device_id_type=MESH,
+        )
+
+    def z_copy(level, shard, d):
+        return in_plane(level, shard, z_send, (level, (d + 1) // 2, shard), (gx, gy + d, ta))
+
+    def x_copy(level, shard, stage):
+        target = (lines[xbits[stage]], gy, ta)
+        return in_plane(level, shard, x_send, (level, stage, shard), target)
+
+    def y_copy(level, shard, sending):
+        size = kept(level)
+        first = (upper if sending else 1 - upper) * size
+        place = weights.at[level, shard, side, pl.ds(pl.multiple_of(first, 16), half - size), :]
+        return pltpu.make_async_remote_copy(
+            src_ref=place,
+            dst_ref=place,
+            send_sem=y_send.at[level, shard],
+            recv_sem=y_recv.at[level, shard],
+            device_id=(gx, gy, twin),
+            device_id_type=MESH,
+        )
+
+    def core_copy(level, shard, kind, mine):
+        size = kept(level)
+        if kind == 0:
+            rows_at = in_rows(level)
+        else:
+            rows_at = pl.ds(pl.multiple_of((1 - upper) * size, 16), half - size)
+        place = weights.at[level, shard, side if mine else 1 - side, rows_at, :]
+        return pltpu.make_async_remote_copy(
+            src_ref=place,
+            dst_ref=place,
+            send_sem=core_send.at[level, kind, shard],
+            recv_sem=core_recv.at[level, kind, shard],
             device_id=of_ta(1),
             device_id_type=MESH,
         )
 
-    def pump(level, stage):
-        if stage == 0:
+    def hops(offset, k):
+        return k + 1 + bin(offset).count("1")
+
+    def has_twin(level):
+        return kept(level) < half
+
+    def forward(level, offset, d, k):
+        shard = shard_id(offset, d, k)
+        valid = inside(d, k)
+        own_shard = offset == 0 and k < 0
+
+        def body():
+            if not own_shard:
+                in_plane(level, shard, ag_send, 0, of_ta(1)).wait_recv()
+                launch(None, lambda: core_copy(level, shard, 0, True), valid)
+            if offset == 0:
+                for way in (1, -1) if k < 0 else (d,):
+                    launch(ahead[way], lambda way=way: z_copy(level, shard, way), valid)
+            for stage in range(stage_of[offset] + 1, len(xbits)):
+                launch(None, lambda stage=stage: x_copy(level, shard, stage), valid)
+            if has_twin(level) and not own_shard:
+                launch(None, lambda: y_copy(level, shard, True), valid)
+
+        guarded(valid, body)
+
+    def crossed(level, offset, d, k):
+        shard = shard_id(offset, d, k)
+
+        def body():
+            y_copy(level, shard, False).wait_recv()
+            launch(None, lambda: core_copy(level, shard, 1, True), inside(d, k))
+
+        guarded(inside(d, k), body)
+
+    last_round = n_gy - 1 + len(xbits) + 1
+
+    def pump(level, step):
+        if step == 0:
             for copy in own(level):
                 copy.wait()
-        for offset in order:
-            if stage_of[offset] != stage - 1:
+        for offset, d, k in shards:
+            if has_twin(level) and hops(offset, k) == step - 1 and (offset or k >= 0):
+                crossed(level, offset, d, k)
+            if hops(offset, k) == step:
+                forward(level, offset, d, k)
+
+    pumped = {}
+
+    def pumps(point):
+        for level, upto in SCHEDULE.get(point, ()):
+            if level < level_count:
+                pump_to(level, min(upto, last_round))
+
+    def pump_to(level, upto):
+        while pumped.get(level, -1) < upto:
+            pumped[level] = pumped.get(level, -1) + 1
+            pump(level, pumped[level])
+
+    def finish(level):
+        pump_to(level, last_round)
+        for offset, d, k in shards:
+            if offset == 0 and k < 0:
                 continue
-            if offset:
-                landed(level, offset).wait_recv()
-                sharing(level, offset, True).start()
-            for later in range(stage, len(bits)):
-                passing(level, offset, later).start()
-
-    stages = len(bits)
-
-    reached = [0]
-
-    def pumps(step):
-        while reached[0] <= step:
-            for level in range(level_count):
-                stage = reached[0] - level
-                if 0 <= stage <= stages:
-                    pump(level, stage)
-            reached[0] += 1
-
-    def finish(level):
-        for offset in order[1:]:
-            sharing(level, offset, False).wait_recv()
+
+            def body():
+                core_copy(level, shard_id(offset, d, k), 0, False).wait_recv()
+                if has_twin(level):
+                    core_copy(level, shard_id(offset, d, k), 1, False).wait_recv()
+
+            guarded(inside(d, k), body)
 
     def regroup(j):
         return pltpu.make_async_remote_copy(
@@ -268,7 +380,7 @@
         select[level + 1] = selection(pairs[pl.ds(level, 1), :])
 
     pl.semaphore_wait(barrier, n_ta - 1 + groups - 1)
-    pumps(0)
+    pumps("start")
 
     for j in near:
         loading(j).wait()
@@ -286,11 +398,12 @@
         lax.fori_loop(0, boxes // BLOCK_BOXES, interpolate, 0, unroll=4)
         if j:
             regroup(j).start()
-
-    pumps(1)
+        pumps(f"interp{j}")
+
     table_copy.wait()
     for j in range(n_ta):
         if j:
+            pumps(f"table{j}")
             regroup(j).wait_recv()
         first = pl.multiple_of(flip(ta, j, n_ta) * span, span)
         for c in range(CHEB):
@@ -306,7 +419,7 @@
     for offset in range(groups - 1, 0, -1):
         moving(offset, True).start()
     arrived[group] = points[group]
-    pumps(2)
+    pumps("spread")
     for offset in range(1, groups):
         moving(offset, False).wait_recv()
 
@@ -325,7 +438,6 @@
         return piece.reshape(chunk, chunk)
 
     for level in range(level_count):
-        pumps(level + stages)
         finish(level)
 
         def own_part(n, carry):
@@ -340,6 +452,7 @@
 
         lax.fori_loop(0, chunks, own_part, 0)
         for k in range(chunks):
+            pumps(f"level{level}.{k}")
             exchange(level, k).wait_recv()
             aligned = jnp.dot(
                 select[level + 1], partner[level, k], preferred_element_type=jnp.float32
@@ -373,9 +486,8 @@
     for level in range(level_count):
         for k in range(chunks):
             exchange(level, k).wait_send()
-        for offset in order[1:]:
-            landed(level, offset).wait_send()
-            sharing(level, offset, True).wait_send()
+    for outer, condition, make in started:
+        guarded(both(outer, condition), lambda: make().wait_send())
 
 
 def on_device(sizes, traces, interp, translations, leaf_slot, pairing):
@@ -413,10 +525,14 @@
             dma((n_ta,)),
             dma,
             dma((levels, 2)),
+            dma((1,)),
+            dma((levels, groups)),
+            dma((levels, 2, groups)),
+            dma((levels, max(1, n_gx.bit_length() - 1), groups)),
             dma((levels, groups)),
             dma((levels, groups)),
-            dma((levels, groups)),
-            dma((levels, groups)),
+            dma((levels, 2, groups)),
+            dma((levels, 2, groups)),
             dma((n_ta,)),
             dma((n_ta,)),
             dma((groups,)),

time: 127 us -> 124 us (0.976)
  Pallas kernels: 124 us -> 122 us
    pallas_call x1, Pallas kernels: 124 us -> 122 us  [on_device(): pl.pallas_call(functools.partial(kernel, sizes), out_shape=jax.ShapeDtype...]
where the time goes in v1:
time: 124 us
  Pallas kernels  122 us (98%)
  local copies, waits for them, and re-layouts  1.87 us (2%)
    pallas_call x1, Pallas kernels, on_device(): pl.pallas_call(functools.partial(kernel, sizes), out_shape=jax.ShapeDtype...  122 us

profile of v1, /device:TPU:0, one launch (start us, length us, event | category | flops | bytes accessed | tf_op | source)
XLA Modules:
  0.0 123.6 jit_solution(3314624981678660686)
XLA Ops:
  0.0 121.7 %shard_map.64 = bf16[256,1024]{1,0:T(8,128)(2,1)} custom-call(bf16[16384,256]{1,0:T(8,128)(2,1)} %traces.1, bf16[2,16]{1,0:T(2,128)(2,1)} %interp.1, bf16[4,256,1024]{2,1,0:T(8,128)(2,1)} %translations.1, s32[1,256]{1,0:T(1,128)} %bitcast.1, s32[4,256]{1,0:T(4,128)} %pairs.1, bf16[1024,512]{1,0:T(8,128)(2,1)} %constant.2.clone.table), custom_call_target="tpu_custom_call" | custom-call | tf_op jit(solution)/shard_map/pallas_call | solution.py:507
  121.7 1.9 %copy.8 = bf16[256,1024]{1,0:T(8,128)(2,1)} copy(bf16[256,1024]{1,0:T(8,128)(2,1)} %shard_map.64) | data formatting | bytes 1048576

commit v2 on v1

--- a/solution.py
+++ b/solution.py
@@ -15,17 +15,59 @@
 BLOCK_BOXES = 16
 TILE = 256
 MESH = pl.DeviceIdType.MESH
-KEPT = (0.625, 0.625, 0.75, 0.75)
+KEPT = (0.5, 0.75, 1, 0.5)
 SCHEDULE = {
-    "start": ((0, 0), (1, 0)),
-    "interp0": ((0, 1),),
-    "table2": ((1, 1),),
-    "spread": ((0, 2), (2, 0), (1, 1), (0, 3), (1, 2), (0, 4), (2, 1)),
-    "level0.0": ((1, 3), (3, 0)),
-    "level1.0": ((2, 2), (3, 1)),
-    "level1.1": ((2, 3),),
-    "level1.2": ((3, 2),),
-    "level2.0": ((3, 3),),
+    "start": ((0, 0, 0, -1),),
+    "interp1": ((0, 1, 0, -1), (0, 0, 0, 0), (0, 1, 0, 0),),
+    "interp3": ((0, 0, 0, 1), (1, 0, 0, 0), (1, 1, 0, 0), (0, 1, 0, 1), (0, 0, 0, 2),),
+    "table2": ((0, 0, 1, 0), (0, 0, 1, 2),),
+    "spread2": (
+        (0, 0, 1, 1),
+        (1, 2, 1, 2),
+        (0, 1, 0, 2),
+        (1, 0, 0, 2),
+        (1, 2, 0, 2),
+        (1, 2, 1, 0),
+    ),
+    "table3": ((1, 0, 1, 0),),
+    "spread3": (
+        (0, 2, 0, -1),
+        (0, 0, 1, -1),
+        (0, 1, 1, -1),
+        (1, 0, 1, 1),
+        (1, 2, 0, 1),
+        (0, 1, 1, 0),
+        (0, 1, 1, 1),
+    ),
+    "spread": ((1, 0, 0, 1), (1, 1, 0, 1), (0, 3, 0, -1), (0, 1, 1, 2), (1, 0, 1, 2),),
+    "own0": ((1, 0, 1, -1),),
+    "level0.1": ((0, 2, 0, 0),),
+    "own1": (
+        (1, 1, 1, 0),
+        (0, 2, 1, -1),
+        (0, 2, 0, 1),
+        (1, 1, 1, -1),
+        (1, 1, 0, 2),
+        (1, 1, 1, 2),
+        (1, 1, 1, 1),
+    ),
+    "level1.0": ((1, 2, 1, -1),),
+    "level1.2": ((0, 2, 0, 2), (0, 3, 0, 0),),
+    "level1.3": ((0, 2, 1, 0),),
+    "own2": ((0, 2, 1, 1), (0, 3, 0, 1), (1, 2, 0, 0), (1, 2, 1, 1), (0, 2, 1, 2),),
+    "level2.0": ((0, 3, 1, -1),),
+    "level2.1": ((1, 3, 0, 1),),
+    "level2.3": ((0, 3, 1, 1), (1, 3, 0, 0),),
+    "own3": (
+        (0, 3, 1, 0),
+        (1, 3, 1, -1),
+        (0, 3, 0, 2),
+        (1, 3, 0, 2),
+        (0, 3, 1, 2),
+        (1, 3, 1, 2),
+        (1, 3, 1, 1),
+        (1, 3, 1, 0),
+    ),
 }
 
 
@@ -234,9 +276,6 @@
             device_id_type=MESH,
         )
 
-    def hops(offset, k):
-        return k + 1 + bin(offset).count("1")
-
     def has_twin(level):
         return kept(level) < half
 
@@ -268,49 +307,65 @@
 
         guarded(inside(d, k), body)
 
-    last_round = n_gy - 1 + len(xbits) + 1
-
-    def pump(level, step):
-        if step == 0:
+    handled = set()
+
+    def piece(across, level, over, k):
+        if (across, level, over, k) in handled or level >= level_count or k > n_gy - 2:
+            return
+        handled.add((across, level, over, k))
+        if not (across or over) and k >= 0:
+            piece(0, level, 0, k - 1)
+        if across and not has_twin(level):
+            return
+        if k < 0 and not (across or over):
             for copy in own(level):
                 copy.wait()
-        for offset, d, k in shards:
-            if has_twin(level) and hops(offset, k) == step - 1 and (offset or k >= 0):
-                crossed(level, offset, d, k)
-            if hops(offset, k) == step:
-                forward(level, offset, d, k)
-
-    pumped = {}
+        for offset, d, at in shards:
+            if at == k and (offset > 0) == (over > 0):
+                if not across:
+                    forward(level, offset, d, k)
+                elif offset or k >= 0:
+                    crossed(level, offset, d, k)
 
     def pumps(point):
-        for level, upto in SCHEDULE.get(point, ()):
-            if level < level_count:
-                pump_to(level, min(upto, last_round))
-
-    def pump_to(level, upto):
-        while pumped.get(level, -1) < upto:
-            pumped[level] = pumped.get(level, -1) + 1
-            pump(level, pumped[level])
-
-    def finish(level):
-        pump_to(level, last_round)
-        for offset, d, k in shards:
-            if offset == 0 and k < 0:
-                continue
+        for entry in SCHEDULE.get(point, ()):
+            piece(*entry)
+
+    def flush(level):
+        for across in range(2):
+            for total in range(-1, n_gy):
+                for over in range(2):
+                    if -1 <= total - over < n_gy - 1:
+                        piece(across, level, over, total - over)
+
+    def finish(level, first, count):
+        for shard in range(first, first + count):
 
             def body():
-                core_copy(level, shard_id(offset, d, k), 0, False).wait_recv()
+                core_copy(level, shard, 0, False).wait_recv()
                 if has_twin(level):
-                    core_copy(level, shard_id(offset, d, k), 1, False).wait_recv()
-
-            guarded(inside(d, k), body)
-
-    def regroup(j):
+                    core_copy(level, shard, 1, False).wait_recv()
+
+            pl.when(group != shard)(body)
+
+    portions = min(4, groups)
+    per_portion = groups // portions
+    portion_rows = boxes // portions
+    portion_order = sorted(range(portions), key=lambda c: (-(c % 2), -c))
+
+    def portion(c):
+        return flip(group // per_portion, c, portions)
+
+    def portion_at(c):
+        return pl.multiple_of(portion(c) * portion_rows, portion_rows)
+
+    def regroup(j, c):
+        place = pl.ds(portion_at(c), portion_rows)
         return pltpu.make_async_remote_copy(
-            src_ref=sampled.at[j],
-            dst_ref=slices.at[j],
-            send_sem=ta_send.at[j],
-            recv_sem=ta_recv.at[j],
+            src_ref=sampled.at[j, :, place, :],
+            dst_ref=slices.at[j, :, place, :],
+            send_sem=ta_send.at[j, c],
+            recv_sem=ta_recv.at[j, c],
             device_id=of_ta(j),
             device_id_type=MESH,
         )
@@ -382,42 +437,46 @@
     pl.semaphore_wait(barrier, n_ta - 1 + groups - 1)
     pumps("start")
 
-    for j in near:
-        loading(j).wait()
-        where = sampled if j else slices
-
-        def interpolate(i, carry):
-            traces_block = tr[j, pl.ds(pl.multiple_of(i * columns, columns), columns), :]
-            both = jnp.dot(mat[...], traces_block, preferred_element_type=jnp.float32)
-            both = both.astype(jnp.bfloat16)
-            place = pl.ds(pl.multiple_of(i * BLOCK_BOXES, BLOCK_BOXES), BLOCK_BOXES)
-            for c in range(CHEB):
-                where[j, c, place, :] = both[c * BLOCK_BOXES : (c + 1) * BLOCK_BOXES, :]
-            return carry
-
-        lax.fori_loop(0, boxes // BLOCK_BOXES, interpolate, 0, unroll=4)
-        if j:
-            regroup(j).start()
-        pumps(f"interp{j}")
+    for turn, c in enumerate(portion_order):
+        for j in near:
+            if turn == 0:
+                loading(j).wait()
+            where = sampled if j else slices
+            for i in range(portion_rows // BLOCK_BOXES):
+                box = pl.multiple_of(portion_at(c) + i * BLOCK_BOXES, BLOCK_BOXES)
+                traces_block = tr[j, pl.ds(pl.multiple_of(box * BOXT, columns), columns), :]
+                pair = jnp.dot(mat[...], traces_block, preferred_element_type=jnp.float32)
+                pair = pair.astype(jnp.bfloat16)
+                for q in range(CHEB):
+                    where[j, q, pl.ds(box, BLOCK_BOXES), :] = pair[
+                        q * BLOCK_BOXES : (q + 1) * BLOCK_BOXES, :
+                    ]
+            if j:
+                regroup(j, c).start()
+        pumps(f"interp{turn}")
 
     table_copy.wait()
-    for j in range(n_ta):
-        if j:
-            pumps(f"table{j}")
-            regroup(j).wait_recv()
-        first = pl.multiple_of(flip(ta, j, n_ta) * span, span)
-        for c in range(CHEB):
-            part = jnp.dot(
-                slices[j, c], fourier[pl.ds(first, span), :], preferred_element_type=jnp.float32
+    for turn, c in enumerate(portion_order):
+        pumps(f"table{turn}")
+        place = pl.ds(portion_at(c), portion_rows)
+        total = jnp.zeros((CHEB * portion_rows, 2 * NF), jnp.float32)
+        for j in range(n_ta):
+            if j:
+                regroup(j, c).wait_recv()
+            first = pl.multiple_of(flip(ta, j, n_ta) * span, span)
+            part = slices[j, :, place, :].reshape(CHEB * portion_rows, span)
+            total += jnp.dot(part, fourier[pl.ds(first, span), :], preferred_element_type=jnp.float32)
+        mine = pl.ds(portion(c) * per_portion, per_portion)
+        for q in range(CHEB):
+            points[mine, :, q * 2 * NF : (q + 1) * 2 * NF] = (
+                total[q * portion_rows : (q + 1) * portion_rows, :]
+                .reshape(per_portion, boxes // groups, 2 * NF)
+                .astype(jnp.bfloat16)
             )
-            cols = pl.ds(c * 2 * NF, 2 * NF)
-            if j:
-                acc[:, cols] += part
-            else:
-                acc[:, cols] = part
-    points[...] = acc[...].reshape(points.shape).astype(jnp.bfloat16)
-    for offset in range(groups - 1, 0, -1):
-        moving(offset, True).start()
+        for offset in range((c + 1) * per_portion - 1, c * per_portion - 1, -1):
+            if offset:
+                moving(offset, True).start()
+        pumps(f"spread{turn}")
     arrived[group] = points[group]
     pumps("spread")
     for offset in range(1, groups):
@@ -438,7 +497,9 @@
         return piece.reshape(chunk, chunk)
 
     for level in range(level_count):
-        finish(level)
+        pumps(f"own{level}")
+        flush(level)
+        finish(level, 0, chunks * per_chunk)
 
         def own_part(n, carry):
             cols = pl.ds(pl.multiple_of(n * chunk, chunk), chunk)
@@ -453,6 +514,7 @@
         lax.fori_loop(0, chunks, own_part, 0)
         for k in range(chunks):
             pumps(f"level{level}.{k}")
+            finish(level, (chunks + k) * per_chunk, per_chunk)
             exchange(level, k).wait_recv()
             aligned = jnp.dot(
                 select[level + 1], partner[level, k], preferred_element_type=jnp.float32
@@ -480,7 +542,8 @@
                         out[:, cols] = total.astype(jnp.bfloat16)
 
     for j in range(1, n_ta):
-        regroup(j).wait_send()
+        for c in range(portions):
+            regroup(j, c).wait_send()
     for offset in range(1, groups):
         moving(offset, True).wait_send()
     for level in range(level_count):
@@ -533,8 +596,8 @@
             dma((levels, groups)),
             dma((levels, 2, groups)),
             dma((levels, 2, groups)),
-            dma((n_ta,)),
-            dma((n_ta,)),
+            dma((n_ta, min(4, groups))),
+            dma((n_ta, min(4, groups))),
             dma((groups,)),
             dma((groups,)),
             dma((levels, chunks)),

time: 124 us -> 109 us (0.88); the launches traced: 124 us -> 107 us
  Pallas kernels: 122 us -> 105 us
    pallas_call x1, Pallas kernels: 122 us -> 105 us  [on_device(): pl.pallas_call(functools.partial(kernel, sizes), out_shape=jax.ShapeDtype...]
where the time goes in v2:
time: 109 us; the launch traced here: 107 us
  Pallas kernels  105 us (96%)
  local copies, waits for them, and re-layouts  1.87 us (2%)
    pallas_call x1, Pallas kernels, on_device(): pl.pallas_call(functools.partial(kernel, sizes), out_shape=jax.ShapeDtype...  105 us

profile of v2, /device:TPU:0, one launch (start us, length us, event | category | flops | bytes accessed | tf_op | source)
XLA Modules:
  0.0 107.1 jit_solution(2198569720929851966)
XLA Ops:
  0.0 105.3 %shard_map.64 = bf16[256,1024]{1,0:T(8,128)(2,1)} custom-call(bf16[16384,256]{1,0:T(8,128)(2,1)} %traces.1, bf16[2,16]{1,0:T(2,128)(2,1)} %interp.1, bf16[4,256,1024]{2,1,0:T(8,128)(2,1)} %translations.1, s32[1,256]{1,0:T(1,128)} %bitcast.1, s32[4,256]{1,0:T(4,128)} %pairs.1, bf16[1024,512]{1,0:T(8,128)(2,1)} %constant.2.clone.table), custom_call_target="tpu_custom_call" | custom-call | tf_op jit(solution)/shard_map/pallas_call | solution.py:570
  105.3 1.9 %copy.8 = bf16[256,1024]{1,0:T(8,128)(2,1)} copy(bf16[256,1024]{1,0:T(8,128)(2,1)} %shard_map.64) | data formatting | bytes 1048576

commit v3 on v2

--- a/solution.py
+++ b/solution.py
@@ -15,59 +15,38 @@
 BLOCK_BOXES = 16
 TILE = 256
 MESH = pl.DeviceIdType.MESH
-KEPT = (0.5, 0.75, 1, 0.5)
+KEPT = (0.625, 0.5, 0.75, 1)
 SCHEDULE = {
-    "start": ((0, 0, 0, -1),),
-    "interp1": ((0, 1, 0, -1), (0, 0, 0, 0), (0, 1, 0, 0),),
-    "interp3": ((0, 0, 0, 1), (1, 0, 0, 0), (1, 1, 0, 0), (0, 1, 0, 1), (0, 0, 0, 2),),
-    "table2": ((0, 0, 1, 0), (0, 0, 1, 2),),
-    "spread2": (
+    "start": ((1, 1, 1, 0), (0, 0, 0, -1),),
+    "interp1": ((0, 1, 0, -1), (1, 2, 0, 2), (0, 0, 0, 0), (1, 1, 1, -1),),
+    "table1": ((0, 0, 0, 2),),
+    "spread1": ((1, 2, 1, -1), (0, 0, 1, -1),),
+    "table2": ((0, 0, 1, 0),),
+    "spread2": ((0, 0, 1, 2), (1, 2, 0, 1), (1, 1, 0, 1), (1, 0, 0, 2), (0, 0, 0, 1),),
+    "table3": ((0, 1, 1, -1), (1, 1, 0, 0), (1, 3, 1, 2), (1, 1, 1, 2), (1, 3, 0, 2),),
+    "spread3": (
+        (0, 1, 0, 0),
         (0, 0, 1, 1),
-        (1, 2, 1, 2),
-        (0, 1, 0, 2),
-        (1, 0, 0, 2),
-        (1, 2, 0, 2),
-        (1, 2, 1, 0),
+        (0, 1, 0, 1),
+        (1, 3, 0, 1),
+        (0, 2, 0, -1),
+        (1, 3, 1, 0),
+        (1, 0, 0, 1),
+        (1, 0, 1, 0),
     ),
-    "table3": ((1, 0, 1, 0),),
-    "spread3": (
-        (0, 2, 0, -1),
-        (0, 0, 1, -1),
-        (0, 1, 1, -1),
-        (1, 0, 1, 1),
-        (1, 2, 0, 1),
-        (0, 1, 1, 0),
-        (0, 1, 1, 1),
-    ),
-    "spread": ((1, 0, 0, 1), (1, 1, 0, 1), (0, 3, 0, -1), (0, 1, 1, 2), (1, 0, 1, 2),),
-    "own0": ((1, 0, 1, -1),),
+    "spread": ((1, 0, 1, -1), (0, 1, 0, 2), (0, 3, 0, -1), (1, 0, 0, 0), (1, 0, 1, 1),),
+    "own0": ((1, 2, 1, 0), (1, 0, 1, 2),),
+    "level0.0": ((1, 2, 1, 1),),
     "level0.1": ((0, 2, 0, 0),),
-    "own1": (
-        (1, 1, 1, 0),
-        (0, 2, 1, -1),
-        (0, 2, 0, 1),
-        (1, 1, 1, -1),
-        (1, 1, 0, 2),
-        (1, 1, 1, 2),
-        (1, 1, 1, 1),
-    ),
-    "level1.0": ((1, 2, 1, -1),),
-    "level1.2": ((0, 2, 0, 2), (0, 3, 0, 0),),
-    "level1.3": ((0, 2, 1, 0),),
-    "own2": ((0, 2, 1, 1), (0, 3, 0, 1), (1, 2, 0, 0), (1, 2, 1, 1), (0, 2, 1, 2),),
-    "level2.0": ((0, 3, 1, -1),),
-    "level2.1": ((1, 3, 0, 1),),
-    "level2.3": ((0, 3, 1, 1), (1, 3, 0, 0),),
-    "own3": (
-        (0, 3, 1, 0),
-        (1, 3, 1, -1),
-        (0, 3, 0, 2),
-        (1, 3, 0, 2),
-        (0, 3, 1, 2),
-        (1, 3, 1, 2),
-        (1, 3, 1, 1),
-        (1, 3, 1, 0),
-    ),
+    "level0.2": ((1, 3, 0, 0),),
+    "level0.3": ((0, 1, 1, 0),),
+    "own1": ((0, 2, 0, 1), (0, 1, 1, 1), (1, 1, 0, 2), (1, 1, 1, 1), (0, 1, 1, 2),),
+    "level1.0": ((0, 2, 0, 2), (0, 3, 0, 0), (0, 2, 1, -1),),
+    "level1.1": ((1, 3, 1, 1),),
+    "level1.2": ((1, 2, 1, 2),),
+    "own2": ((0, 2, 1, 0), (0, 3, 1, -1), (0, 3, 0, 1), (0, 2, 1, 1), (0, 2, 1, 2), (1, 2, 0, 0),),
+    "level2.2": ((1, 3, 1, -1), (0, 3, 1, 0),),
+    "own3": ((0, 3, 0, 2), (0, 3, 1, 2), (0, 3, 1, 1),),
 }
 
 
@@ -88,6 +67,25 @@
             result = result + bit - 2 * bit * ((index // bit) % 2)
         bit *= 2
     return result
+
+
+def mask_of(level, levels, devices):
+    return 2 ** (level * (devices.bit_length() - 1) // levels)
+
+
+def halves_join(sizes, levels, rows, width):
+    n_gx, n_gy, n_ta = sizes
+    devices = n_gx * n_gy * n_ta
+    return (
+        levels == 4
+        and n_ta >= 4
+        and mask_of(1, levels, devices) == 2
+        and mask_of(2, levels, devices) >= n_ta
+        and rows >= TILE
+        and rows == max(TILE, rows)
+        and width // rows >= 2
+        and rows * n_gx * n_gy == 2 * width
+    )
 
 
 def kernel(
@@ -111,6 +109,16 @@
     states,
     partner,
     select,
+    narrow,
+    short,
+    pairs_twin,
+    select_twin,
+    turned,
+    both_states,
+    both_partner,
+    sums,
+    part_out,
+    part_in,
     load_sem,
     table_sem,
     own_sem,
@@ -128,6 +136,11 @@
     g_recv,
     level_send,
     level_recv,
+    pairs_sem,
+    join_send,
+    join_recv,
+    part_send,
+    part_recv,
 ):
     n_gx, n_gy, n_ta = sizes
     groups = n_gx * n_gy
@@ -158,12 +171,44 @@
             traces.at[pl.ds(pl.multiple_of(t * block, block), block), :], tr.at[j], load_sem.at[j]
         )
 
+    upper = (ta // 2) % 2
+    joined = halves_join(sizes, level_count, rows, width)
+
     def own(level):
+        if joined and level == 1:
+            strip = chunk // 2
+            return [
+                pltpu.make_async_copy(
+                    translations.at[
+                        level,
+                        pl.ds(part * half, half),
+                        pl.ds(pl.multiple_of(k * chunk + upper * strip, strip), strip),
+                    ],
+                    narrow.at[group, part, :, pl.ds(k * strip, strip)],
+                    own_sem.at[level, part, k],
+                )
+                for part in range(2)
+                for k in range(chunks)
+            ]
+        if joined and level == 2:
+            quarter = half // 2
+            return [
+                pltpu.make_async_copy(
+                    translations.at[
+                        level,
+                        pl.ds(pl.multiple_of(upper * half + part * quarter, quarter), quarter),
+                        :,
+                    ],
+                    short.at[group, part],
+                    own_sem.at[level, part, 0],
+                )
+                for part in range(2)
+            ]
         return [
             pltpu.make_async_copy(
                 translations.at[level, pl.ds(part * half, half), :],
                 weights.at[level, group, part],
-                own_sem.at[level, part],
+                own_sem.at[level, part, 0],
             )
             for part in range(2)
         ]
@@ -186,10 +231,9 @@
     ]
     twins = n_ta >= 4
     twin = flip(ta, 2, n_ta) if twins else ta
-    upper = (ta // 2) % 2
 
     def kept(level):
-        if not twins:
+        if not twins or (joined and level in (1, 2)):
             return half
         return max(half // 2, round(half * KEPT[level % len(KEPT)] / 16) * 16)
 
@@ -229,8 +273,15 @@
             return pl.ds(0, half)
         return pl.ds(pl.multiple_of(upper * (half - size), 16), size)
 
+    def held(level, shard, part):
+        if joined and level == 1:
+            return narrow.at[shard, part]
+        if joined and level == 2:
+            return short.at[shard, part]
+        return weights.at[level, shard, part, in_rows(level), :]
+
     def in_plane(level, shard, sem_ref, sem_at, target):
-        place = weights.at[level, shard, side, in_rows(level), :]
+        place = held(level, shard, side)
         return pltpu.make_async_remote_copy(
             src_ref=place,
             dst_ref=place,
@@ -262,11 +313,12 @@
 
     def core_copy(level, shard, kind, mine):
         size = kept(level)
+        part = side if mine else 1 - side
         if kind == 0:
-            rows_at = in_rows(level)
+            place = held(level, shard, part)
         else:
             rows_at = pl.ds(pl.multiple_of((1 - upper) * size, 16), half - size)
-        place = weights.at[level, shard, side if mine else 1 - side, rows_at, :]
+            place = weights.at[level, shard, part, rows_at, :]
         return pltpu.make_async_remote_copy(
             src_ref=place,
             dst_ref=place,
@@ -394,6 +446,32 @@
             device_id_type=MESH,
         )
 
+    def twin_copy(src, dst, sems):
+        return pltpu.make_async_remote_copy(
+            src_ref=src,
+            dst_ref=dst,
+            send_sem=sems[0],
+            recv_sem=sems[1],
+            device_id=of_ta(2),
+            device_id_type=MESH,
+        )
+
+    def pairs_copy():
+        return twin_copy(pairs, pairs_twin, (pairs_sem.at[0], pairs_sem.at[1]))
+
+    def handing(n):
+        return twin_copy(part_out.at[n], part_in.at[n], (part_send.at[n], part_recv.at[n]))
+
+    def join(r, n):
+        return pltpu.make_async_remote_copy(
+            src_ref=both_states.at[r, n],
+            dst_ref=both_partner.at[r, n],
+            send_sem=join_send.at[r, n],
+            recv_sem=join_recv.at[r, n],
+            device_id=of_group(mask_of(2, level_count, groups * n_ta) // n_ta),
+            device_id_type=MESH,
+        )
+
     near = [n_ta - 1 - j for j in range(n_ta)]
     for j in near:
         loading(j).start()
@@ -436,6 +514,8 @@
 
     pl.semaphore_wait(barrier, n_ta - 1 + groups - 1)
     pumps("start")
+    if joined:
+        pairs_copy().start()
 
     for turn, c in enumerate(portion_order):
         for j in near:
@@ -478,6 +558,10 @@
                 moving(offset, True).start()
         pumps(f"spread{turn}")
     arrived[group] = points[group]
+    if joined:
+        pairs_copy().wait_recv()
+        for level in (1, 2):
+            select_twin[level - 1] = selection(pairs_twin[pl.ds(level, 1), :])
     pumps("spread")
     for offset in range(1, groups):
         moving(offset, False).wait_recv()
@@ -496,7 +580,108 @@
         piece = weights[level, k * per_chunk : (k + 1) * per_chunk, :, :, cols]
         return piece.reshape(chunk, chunk)
 
-    for level in range(level_count):
+    def dots(left, right):
+        return jnp.dot(left, right, preferred_element_type=jnp.float32)
+
+    def columns_of(n):
+        return pl.ds(pl.multiple_of(n * chunk, chunk), chunk)
+
+    def first_joined(level):
+        pumps(f"own{level}")
+        flush(level)
+        finish(level, 0, 2 * chunks * per_chunk)
+
+        def piece_of(k, cols):
+            return narrow[k, :, :, cols].reshape(chunk, chunk)
+
+        for k in range(chunks):
+            turned[k] = dots(select_twin[level - 1], states[level, k]).astype(jnp.bfloat16)
+
+        def own_part(n, carry):
+            cols = columns_of(n)
+            straight = jnp.zeros((boxes, chunk), jnp.float32)
+            for k in range(chunks):
+                straight += dots(states[level, k], piece_of(k, cols))
+            sums[0, :, cols] = straight
+            across = jnp.zeros((boxes, chunk), jnp.float32)
+            for k in range(chunks):
+                across += dots(turned[k], piece_of(chunks + k, cols))
+            sums[1, :, cols] = across
+            return carry
+
+        lax.fori_loop(0, chunks // 2, own_part, 0)
+        for k in range(chunks):
+            pumps(f"level{level}.{k}")
+            exchange(level, k).wait_recv()
+            aligned = dots(select[level + 1], partner[level, k]).astype(jnp.bfloat16)
+            if k < chunks - 1:
+
+                def partner_part(n, carry):
+                    cols = columns_of(n)
+                    sums[1, :, cols] += dots(partner[level, k], piece_of(k, cols))
+                    sums[0, :, cols] += dots(aligned, piece_of(chunks + k, cols))
+                    return carry
+
+                lax.fori_loop(0, chunks // 2, partner_part, 0)
+            else:
+                for r in (1, 0):
+                    for n in range(chunks // 2):
+                        cols = pl.ds(n * chunk, chunk)
+                        if r:
+                            last = dots(partner[level, k], piece_of(k, cols))
+                        else:
+                            last = dots(aligned, piece_of(chunks + k, cols))
+                        both_states[r, n] = (sums[r, :, cols] + last).astype(jnp.bfloat16)
+                        join(r, n).start()
+
+    def second_joined(level):
+        pumps(f"own{level}")
+        flush(level)
+        finish(level, 0, 2 * chunks * per_chunk)
+
+        def piece_of(n, cols):
+            return short[2 * n : 2 * n + 2, :, :, cols].reshape(chunk, chunk)
+
+        for r in (1, 0):
+
+            def own_part(q, carry):
+                cols = columns_of(q)
+                total = jnp.zeros((boxes, chunk), jnp.float32)
+                for n in range(chunks // 2):
+                    total += dots(both_states[r, n], piece_of(n, cols))
+                sums[r, :, cols] = total
+                return carry
+
+            lax.fori_loop(0, chunks, own_part, 0)
+        turns = [(r, n) for r in (1, 0) for n in range(chunks // 2)]
+        for turn, (r, n) in enumerate(turns):
+            if turn < chunks:
+                pumps(f"level{level}.{turn}")
+            join(r, n).wait_recv()
+            table_of = select_twin[level - 1] if r else select[level + 1]
+            aligned = dots(table_of, both_partner[r, n]).astype(jnp.bfloat16)
+            if n < chunks // 2 - 1:
+
+                def partner_part(q, carry):
+                    cols = columns_of(q)
+                    sums[r, :, cols] += dots(aligned, piece_of(chunks // 2 + n, cols))
+                    return carry
+
+                lax.fori_loop(0, chunks, partner_part, 0)
+                continue
+            for q in range(chunks):
+                cols = pl.ds(q * chunk, chunk)
+                total = sums[r, :, cols] + dots(aligned, piece_of(chunks // 2 + n, cols))
+                if r:
+                    part_out[q] = total.astype(jnp.bfloat16)
+                    handing(q).start()
+                else:
+                    handing(q).wait_recv()
+                    total += part_in[q].astype(jnp.float32)
+                    states[level + 1, q] = total.astype(jnp.bfloat16)
+                    exchange(level + 1, q).start()
+
+    def plain_level(level):
         pumps(f"own{level}")
         flush(level)
         finish(level, 0, chunks * per_chunk)
@@ -541,6 +726,12 @@
                     else:
                         out[:, cols] = total.astype(jnp.bfloat16)
 
+    for level in range(level_count):
+        if joined and level in (1, 2):
+            (first_joined if level == 1 else second_joined)(level)
+        else:
+            plain_level(level)
+
     for j in range(1, n_ta):
         for c in range(portions):
             regroup(j, c).wait_send()
@@ -548,7 +739,15 @@
         moving(offset, True).wait_send()
     for level in range(level_count):
         for k in range(chunks):
-            exchange(level, k).wait_send()
+            if not (joined and level == 2):
+                exchange(level, k).wait_send()
+    if joined:
+        pairs_copy().wait_send()
+        for n in range(chunks):
+            handing(n).wait_send()
+        for r in range(2):
+            for n in range(chunks // 2):
+                join(r, n).wait_send()
     for outer, condition, make in started:
         guarded(both(outer, condition), lambda: make().wait_send())
 
@@ -564,6 +763,11 @@
     chunks = width // chunk
     table = jnp.asarray(spectrum_table(span * n_ta, NF))
     bf16, f32 = jnp.bfloat16, jnp.float32
+    joined = halves_join(sizes, levels, rows, width)
+
+    def extra(shape, kind):
+        return pltpu.VMEM(shape if joined else (1,) * (len(shape) - 2) + (16, 128), kind)
+
     anywhere = pl.BlockSpec(memory_space=pl.ANY)
     vmem = pl.BlockSpec(memory_space=pltpu.VMEM)
     dma = pltpu.SemaphoreType.DMA
@@ -585,9 +789,19 @@
             pltpu.VMEM((levels, chunks, boxes, chunk), bf16),
             pltpu.VMEM((levels, chunks, boxes, chunk), bf16),
             pltpu.VMEM((levels + 1, boxes, boxes), bf16),
+            extra((groups, 2, rows // 2, width // 2), bf16),
+            extra((groups, 2, rows // 4, width), bf16),
+            extra((levels, boxes), jnp.int32),
+            extra((2, boxes, boxes), bf16),
+            extra((chunks, boxes, chunk), bf16),
+            extra((2, chunks // 2, boxes, chunk), bf16),
+            extra((2, chunks // 2, boxes, chunk), bf16),
+            extra((2, boxes, width), f32),
+            extra((chunks, boxes, chunk), bf16),
+            extra((chunks, boxes, chunk), bf16),
             dma((n_ta,)),
             dma,
-            dma((levels, 2)),
+            dma((levels, 2, chunks)),
             dma((1,)),
             dma((levels, groups)),
             dma((levels, 2, groups)),
@@ -602,6 +816,11 @@
             dma((groups,)),
             dma((levels, chunks)),
             dma((levels, chunks)),
+            dma((2,)),
+            dma((2, max(1, chunks // 2))),
+            dma((2, max(1, chunks // 2))),
+            dma((chunks,)),
+            dma((chunks,)),
         ],
         compiler_params=pltpu.CompilerParams(
             collective_id=0, has_side_effects=True, vmem_limit_bytes=60 * 2**20

time: 109 us -> 103 us (0.945); the launches traced: 107 us -> 103 us
  Pallas kernels: 105 us -> 101 us
    pallas_call x1, Pallas kernels: 105 us -> 101 us  [on_device(): pl.pallas_call(functools.partial(kernel, sizes), out_shape=jax.ShapeDtype...]
where the time goes in v3:
time: 103 us
  Pallas kernels  101 us (98%)
  local copies, waits for them, and re-layouts  1.87 us (2%)
    pallas_call x1, Pallas kernels, on_device(): pl.pallas_call(functools.partial(kernel, sizes), out_shape=jax.ShapeDtype...  101 us

profile of v3, /device:TPU:0, one launch (start us, length us, event | category | flops | bytes accessed | tf_op | source)
XLA Modules:
  0.0 103.1 jit_solution(8124557697831854630)
XLA Ops:
  0.0 101.2 %shard_map.64 = bf16[256,1024]{1,0:T(8,128)(2,1)} custom-call(bf16[16384,256]{1,0:T(8,128)(2,1)} %traces.1, bf16[2,16]{1,0:T(2,128)(2,1)} %interp.1, bf16[4,256,1024]{2,1,0:T(8,128)(2,1)} %translations.1, s32[1,256]{1,0:T(1,128)} %bitcast.1, s32[4,256]{1,0:T(4,128)} %pairs.1, bf16[1024,512]{1,0:T(8,128)(2,1)} %constant.2.clone.table), custom_call_target="tpu_custom_call" | custom-call | tf_op jit(solution)/shard_map/pallas_call | solution.py:774
  101.2 1.9 %copy.8 = bf16[256,1024]{1,0:T(8,128)(2,1)} copy(bf16[256,1024]{1,0:T(8,128)(2,1)} %shard_map.64) | data formatting | bytes 1048576

commit v4 on v3

--- a/solution.py
+++ b/solution.py
@@ -15,38 +15,46 @@
 BLOCK_BOXES = 16
 TILE = 256
 MESH = pl.DeviceIdType.MESH
-KEPT = (0.625, 0.5, 0.75, 1)
+KEPT = (0.625, 0.5, 0.625, 1)
 SCHEDULE = {
-    "start": ((1, 1, 1, 0), (0, 0, 0, -1),),
-    "interp1": ((0, 1, 0, -1), (1, 2, 0, 2), (0, 0, 0, 0), (1, 1, 1, -1),),
-    "table1": ((0, 0, 0, 2),),
-    "spread1": ((1, 2, 1, -1), (0, 0, 1, -1),),
-    "table2": ((0, 0, 1, 0),),
-    "spread2": ((0, 0, 1, 2), (1, 2, 0, 1), (1, 1, 0, 1), (1, 0, 0, 2), (0, 0, 0, 1),),
-    "table3": ((0, 1, 1, -1), (1, 1, 0, 0), (1, 3, 1, 2), (1, 1, 1, 2), (1, 3, 0, 2),),
+    "start": ((1, 1, 0, 1), (0, 0, 0, -1),),
+    "interp0": ((1, 1, 1, 1),),
+    "interp1": ((0, 1, 0, -1),),
+    "interp3": ((0, 0, 1, -1), (1, 1, 0, 0), (0, 0, 0, 0), (1, 1, 1, -1),),
+    "spread0": ((1, 1, 0, 2), (0, 0, 0, 1), (1, 2, 0, 2), (1, 1, 1, 0),),
+    "table1": ((1, 0, 1, -1),),
+    "spread1": ((1, 2, 1, 0), (0, 0, 0, 2), (1, 3, 1, 2),),
+    "table2": ((1, 2, 1, -1), (0, 0, 1, 0),),
+    "spread2": ((0, 0, 1, 2), (0, 1, 1, -1), (0, 1, 0, 0),),
+    "table3": ((1, 0, 0, 1), (1, 0, 0, 0), (1, 3, 0, 1), (1, 3, 1, 1),),
     "spread3": (
-        (0, 1, 0, 0),
         (0, 0, 1, 1),
+        (1, 0, 0, 2),
+        (0, 2, 0, -1),
+        (1, 0, 1, 0),
+        (1, 0, 1, 2),
         (0, 1, 0, 1),
-        (1, 3, 0, 1),
-        (0, 2, 0, -1),
-        (1, 3, 1, 0),
-        (1, 0, 0, 1),
-        (1, 0, 1, 0),
+        (1, 0, 1, 1),
     ),
-    "spread": ((1, 0, 1, -1), (0, 1, 0, 2), (0, 3, 0, -1), (1, 0, 0, 0), (1, 0, 1, 1),),
-    "own0": ((1, 2, 1, 0), (1, 0, 1, 2),),
-    "level0.0": ((1, 2, 1, 1),),
-    "level0.1": ((0, 2, 0, 0),),
-    "level0.2": ((1, 3, 0, 0),),
-    "level0.3": ((0, 1, 1, 0),),
-    "own1": ((0, 2, 0, 1), (0, 1, 1, 1), (1, 1, 0, 2), (1, 1, 1, 1), (0, 1, 1, 2),),
-    "level1.0": ((0, 2, 0, 2), (0, 3, 0, 0), (0, 2, 1, -1),),
-    "level1.1": ((1, 3, 1, 1),),
-    "level1.2": ((1, 2, 1, 2),),
-    "own2": ((0, 2, 1, 0), (0, 3, 1, -1), (0, 3, 0, 1), (0, 2, 1, 1), (0, 2, 1, 2), (1, 2, 0, 0),),
-    "level2.2": ((1, 3, 1, -1), (0, 3, 1, 0),),
-    "own3": ((0, 3, 0, 2), (0, 3, 1, 2), (0, 3, 1, 1),),
+    "level0.0": ((0, 1, 0, 2), (1, 2, 0, 0), (0, 2, 0, 0), (1, 2, 1, 2),),
+    "level0.2": ((0, 3, 0, -1),),
+    "own1": (
+        (0, 2, 1, -1),
+        (0, 1, 1, 2),
+        (1, 1, 1, 2),
+        (0, 2, 0, 1),
+        (0, 1, 1, 1),
+        (0, 1, 1, 0),
+        (1, 2, 1, 1),
+        (0, 2, 0, 2),
+        (1, 2, 0, 1),
+        (0, 3, 0, 0),
+    ),
+    "own2": ((0, 2, 1, 0), (1, 3, 0, 2), (0, 2, 1, 1), (0, 2, 1, 2), (0, 3, 0, 1),),
+    "level2.0": ((1, 3, 1, 0),),
+    "level2.1": ((1, 3, 1, -1),),
+    "level2.2": ((1, 3, 0, 0), (0, 3, 1, 0),),
+    "own3": ((0, 3, 1, 1), (0, 3, 0, 2), (0, 3, 1, 2), (0, 3, 1, -1),),
 }
 
 
@@ -165,12 +173,6 @@
     def of_ta(offset):
         return (gx, gy, flip(ta, offset, n_ta))
 
-    def loading(j):
-        t = flip(ta, j, n_ta)
-        return pltpu.make_async_copy(
-            traces.at[pl.ds(pl.multiple_of(t * block, block), block), :], tr.at[j], load_sem.at[j]
-        )
-
     upper = (ta // 2) % 2
     joined = halves_join(sizes, level_count, rows, width)
 
@@ -411,6 +413,14 @@
     def portion_at(c):
         return pl.multiple_of(portion(c) * portion_rows, portion_rows)
 
+    def loading(j, c):
+        size = portion_rows * BOXT
+        first = pl.multiple_of(portion(c) * size, size)
+        source = pl.multiple_of(flip(ta, j, n_ta) * block + first, size)
+        return pltpu.make_async_copy(
+            traces.at[pl.ds(source, size), :], tr.at[j, pl.ds(first, size), :], load_sem.at[j, c]
+        )
+
     def regroup(j, c):
         place = pl.ds(portion_at(c), portion_rows)
         return pltpu.make_async_remote_copy(
@@ -473,13 +483,19 @@
         )
 
     near = [n_ta - 1 - j for j in range(n_ta)]
-    for j in near:
-        loading(j).start()
-    for level in range(level_count):
+    table_copy = pltpu.make_async_copy(table, fourier, table_sem)
+    for copy in own(0):
+        copy.start()
+    for turn, c in enumerate(portion_order):
+        for j in near:
+            loading(j, c).start()
+        if turn == 0:
+            table_copy.start()
+            for copy in own(1):
+                copy.start()
+    for level in range(2, level_count):
         for copy in own(level):
             copy.start()
-    table_copy = pltpu.make_async_copy(table, fourier, table_sem)
-    table_copy.start()
 
     barrier = pltpu.get_barrier_semaphore()
     for j in range(1, n_ta):
@@ -519,8 +535,7 @@
 
     for turn, c in enumerate(portion_order):
         for j in near:
-            if turn == 0:
-                loading(j).wait()
+            loading(j, c).wait()
             where = sampled if j else slices
             for i in range(portion_rows // BLOCK_BOXES):
                 box = pl.multiple_of(portion_at(c) + i * BLOCK_BOXES, BLOCK_BOXES)
@@ -799,7 +814,7 @@
             extra((2, boxes, width), f32),
             extra((chunks, boxes, chunk), bf16),
             extra((chunks, boxes, chunk), bf16),
-            dma((n_ta,)),
+            dma((n_ta, min(4, groups))),
             dma,
             dma((levels, 2, chunks)),
             dma((1,)),

time: 103 us -> 103 us (level); the launches traced: 103 us -> 102 us
  Pallas kernels: 101 us -> 99.8 us
    pallas_call x1, Pallas kernels: 101 us -> 99.8 us  [on_device(): pl.pallas_call(functools.partial(kernel, sizes), out_shape=jax.ShapeDtype...]
where the time goes in v4:
time: 103 us; the launch traced here: 102 us
  Pallas kernels  99.8 us (97%)
  local copies, waits for them, and re-layouts  1.87 us (2%)
    pallas_call x1, Pallas kernels, on_device(): pl.pallas_call(functools.partial(kernel, sizes), out_shape=jax.ShapeDtype...  99.8 us

profile of v4, /device:TPU:0, one launch (start us, length us, event | category | flops | bytes accessed | tf_op | source)
XLA Modules:
  0.0 101.7 jit_solution(15186745779293812866)
XLA Ops:
  0.0 99.8 %shard_map.64 = bf16[256,1024]{1,0:T(8,128)(2,1)} custom-call(bf16[16384,256]{1,0:T(8,128)(2,1)} %traces.1, bf16[2,16]{1,0:T(2,128)(2,1)} %interp.1, bf16[4,256,1024]{2,1,0:T(8,128)(2,1)} %translations.1, s32[1,256]{1,0:T(1,128)} %bitcast.1, s32[4,256]{1,0:T(4,128)} %pairs.1, bf16[1024,512]{1,0:T(8,128)(2,1)} %constant.2.clone.table), custom_call_target="tpu_custom_call" | custom-call | tf_op jit(solution)/shard_map/pallas_call | solution.py:789
  99.8 1.9 %copy.8 = bf16[256,1024]{1,0:T(8,128)(2,1)} copy(bf16[256,1024]{1,0:T(8,128)(2,1)} %shard_map.64) | data formatting | bytes 1048576

commit v5 on v4

--- a/solution.py
+++ b/solution.py
@@ -15,46 +15,54 @@
 BLOCK_BOXES = 16
 TILE = 256
 MESH = pl.DeviceIdType.MESH
-KEPT = (0.625, 0.5, 0.625, 1)
+KEPT = (0.625, 0.5, 0.875, 1)
 SCHEDULE = {
-    "start": ((1, 1, 0, 1), (0, 0, 0, -1),),
-    "interp0": ((1, 1, 1, 1),),
-    "interp1": ((0, 1, 0, -1),),
-    "interp3": ((0, 0, 1, -1), (1, 1, 0, 0), (0, 0, 0, 0), (1, 1, 1, -1),),
-    "spread0": ((1, 1, 0, 2), (0, 0, 0, 1), (1, 2, 0, 2), (1, 1, 1, 0),),
-    "table1": ((1, 0, 1, -1),),
-    "spread1": ((1, 2, 1, 0), (0, 0, 0, 2), (1, 3, 1, 2),),
-    "table2": ((1, 2, 1, -1), (0, 0, 1, 0),),
-    "spread2": ((0, 0, 1, 2), (0, 1, 1, -1), (0, 1, 0, 0),),
-    "table3": ((1, 0, 0, 1), (1, 0, 0, 0), (1, 3, 0, 1), (1, 3, 1, 1),),
+    "start": ((0, 0, 0, -1), (1, 2, 0, 1), (1, 3, 0, 1),),
+    "interp0": ((0, 2, 0, -1), (1, 1, 1, -1),),
+    "interp1": ((0, 0, 0, 0),),
+    "interp3": ((1, 1, 0, 1),),
+    "spread0": ((1, 1, 1, 1), (1, 2, 1, 2), (1, 0, 0, 0), (0, 0, 0, 2), (0, 0, 1, 0),),
+    "table1": ((0, 0, 1, -1), (1, 1, 0, 2), (0, 0, 0, 1), (0, 1, 0, -1),),
+    "spread2": (
+        (1, 0, 1, 0),
+        (0, 2, 1, -1),
+        (1, 0, 0, 2),
+        (1, 1, 1, 0),
+        (0, 0, 1, 1),
+        (1, 2, 1, -1),
+        (0, 1, 0, 0),
+        (0, 0, 1, 2),
+    ),
+    "table3": ((1, 0, 0, 1), (1, 3, 1, -1),),
     "spread3": (
-        (0, 0, 1, 1),
-        (1, 0, 0, 2),
-        (0, 2, 0, -1),
-        (1, 0, 1, 0),
+        (1, 3, 1, 1),
+        (0, 1, 0, 1),
+        (1, 3, 0, 0),
         (1, 0, 1, 2),
-        (0, 1, 0, 1),
-        (1, 0, 1, 1),
+        (1, 3, 0, 2),
+        (0, 3, 0, -1),
+        (0, 1, 1, -1),
     ),
-    "level0.0": ((0, 1, 0, 2), (1, 2, 0, 0), (0, 2, 0, 0), (1, 2, 1, 2),),
-    "level0.2": ((0, 3, 0, -1),),
+    "spread": ((1, 0, 1, 1), (1, 0, 1, -1),),
+    "level0.0": ((0, 1, 0, 2),),
+    "level0.3": ((0, 2, 0, 0),),
     "own1": (
-        (0, 2, 1, -1),
+        (0, 1, 1, 0),
         (0, 1, 1, 2),
+        (1, 1, 0, 0),
+        (0, 1, 1, 1),
+        (0, 2, 0, 1),
         (1, 1, 1, 2),
-        (0, 2, 0, 1),
-        (0, 1, 1, 1),
-        (0, 1, 1, 0),
-        (1, 2, 1, 1),
         (0, 2, 0, 2),
-        (1, 2, 0, 1),
-        (0, 3, 0, 0),
     ),
-    "own2": ((0, 2, 1, 0), (1, 3, 0, 2), (0, 2, 1, 1), (0, 2, 1, 2), (0, 3, 0, 1),),
-    "level2.0": ((1, 3, 1, 0),),
-    "level2.1": ((1, 3, 1, -1),),
-    "level2.2": ((1, 3, 0, 0), (0, 3, 1, 0),),
-    "own3": ((0, 3, 1, 1), (0, 3, 0, 2), (0, 3, 1, 2), (0, 3, 1, -1),),
+    "level1.1": ((0, 3, 0, 0), (1, 2, 1, 1),),
+    "level1.2": ((1, 2, 0, 2),),
+    "level1.3": ((1, 3, 1, 2), (1, 2, 1, 0), (1, 2, 0, 0),),
+    "own2": ((0, 2, 1, 1), (0, 2, 1, 0), (0, 2, 1, 2),),
+    "level2.0": ((0, 3, 0, 1),),
+    "level2.2": ((1, 3, 1, 0),),
+    "level2.3": ((0, 3, 1, 0), (0, 3, 1, -1),),
+    "own3": ((0, 3, 1, 1), (0, 3, 0, 2), (0, 3, 1, 2),),
 }
 
 

time: 103 us -> 100 us (0.971); the launches traced: 102 us -> 100 us
  Pallas kernels: 99.8 us -> 98.4 us
    pallas_call x1, Pallas kernels: 99.8 us -> 98.4 us  [on_device(): pl.pallas_call(functools.partial(kernel, sizes), out_shape=jax.ShapeDtype...]
where the time goes in v5:
time: 100 us
  Pallas kernels  98.4 us (98%)
  local copies, waits for them, and re-layouts  1.87 us (2%)
    pallas_call x1, Pallas kernels, on_device(): pl.pallas_call(functools.partial(kernel, sizes), out_shape=jax.ShapeDtype...  98.4 us

profile of v5, /device:TPU:0, one launch (start us, length us, event | category | flops | bytes accessed | tf_op | source)
XLA Modules:
  0.0 100.3 jit_solution(14473102288048486006)
XLA Ops:
  0.0 98.4 %shard_map.64 = bf16[256,1024]{1,0:T(8,128)(2,1)} custom-call(bf16[16384,256]{1,0:T(8,128)(2,1)} %traces.1, bf16[2,16]{1,0:T(2,128)(2,1)} %interp.1, bf16[4,256,1024]{2,1,0:T(8,128)(2,1)} %translations.1, s32[1,256]{1,0:T(1,128)} %bitcast.1, s32[4,256]{1,0:T(4,128)} %pairs.1, bf16[1024,512]{1,0:T(8,128)(2,1)} %constant.2.clone.table), custom_call_target="tpu_custom_call" | custom-call | tf_op jit(solution)/shard_map/pallas_call | solution.py:797
  98.4 1.9 %copy.8 = bf16[256,1024]{1,0:T(8,128)(2,1)} copy(bf16[256,1024]{1,0:T(8,128)(2,1)} %shard_map.64) | data formatting | bytes 1048576
